TPU v7x, 128 devices: a whole 4x4x4 slice. The times are simulated.
128 devices in a mesh: pb: 8 (over x, core), kv: 8 (over z_lo, y), ha: 2 (over z_hi).
Axes of the slice: x: 4, y: 4, z: 4 (z_hi: 2, z_lo: 2; z = z_hi * 2 + z_lo), core: 2. Of those that a mesh axis runs over, the one named last changes fastest.
Arguments:
- queries: bfloat16 [12288, 2048], P(('pb', 'kv', 'ha')), may hold values from -48 to 48
- keys: bfloat16 [12288, 2048], P(('pb', 'kv', 'ha')), may hold values from -6 to 6
- values: bfloat16 [12288, 2048], P(('pb', 'kv', 'ha')), may hold values from -6 to 6
- masked_at: int32 [3072], replicated, may hold values from 0 to 12287, as said below
- mask_query: bfloat16 [2048], replicated, may hold values from -6 to 6
- mask_key: bfloat16 [2048], replicated, may hold values from -6 to 6
- mask_value: bfloat16 [2048], replicated, may hold values from -6 to 6
Outputs:
- attended: bfloat16 [12288, 2048], P(('pb', 'kv', 'ha'))
Inputs may be any that keep to these rules, and one draw needn't show every extreme that they name: `masked_at`: 3072 distinct positions in rising order.
All inputs are finite; a program needn't handle non-finite values.
Results may differ from a plain program's by a relative error of at most 0.006.
Values may be sent and summed in bfloat16 or wider, within the bound.
No kernel may reach another device: no remote copies, remote signals or barrier semaphores. Data moves between devices by JAX's collectives and lax.ppermute only.
A program may use at most 128 MiB of HBM per device.

v0:
```python
import math
import jax
import jax.numpy as jnp
from jax import lax
from jax.sharding import PartitionSpec as P

DH = 128
HEADS = 16
rope_theta = 500000.0
very_negative = -1e30


def side_by_side(arrays, axis, dim, along):
    both = jnp.concatenate(arrays, axis=along)
    whole, at, gathered = (lax.all_gather(both, axis, axis=dim, tiled=True), 0, [])
    for a in arrays:
        gathered.append(lax.slice_in_dim(whole, at, at + a.shape[along], axis=along))
        at += a.shape[along]
    return tuple(gathered)


def rotated(vector, positions):
    halves = DH // 2
    exponent = jnp.arange(halves, dtype=jnp.float32) * (2.0 / DH)
    inverse = 1.0 / rope_theta**exponent
    angles = positions.astype(jnp.float32)[:, None] * inverse[None, :]
    cosine = jnp.cos(angles)[:, None, :]
    sine_part = jnp.sin(angles)[:, None, :]
    per_head = vector.astype(jnp.float32).reshape(HEADS, DH)
    first_half = per_head[None, :, :halves]
    second = per_head[None, :, halves:]
    result = jnp.concatenate(
        [first_half * cosine - second * sine_part, second * cosine + first_half * sine_part], axis=2
    )
    return result.reshape(positions.shape[0], HEADS * DH).astype(jnp.bfloat16)


def attend_piece(running, head_queries, piece_keys, piece_values, score_scale):
    head_total = head_queries.shape[0]

    def per_head(packed):
        head_index, query_part, old_max, old_total, old_sum = packed
        key_part = lax.dynamic_slice_in_dim(piece_keys, head_index * DH, DH, 1)
        value_part = lax.dynamic_slice_in_dim(piece_values, head_index * DH, DH, 1)
        scores = (
            jnp.einsum("qd,kd->qk", query_part, key_part, preferred_element_type=jnp.float32)
            * score_scale
        )
        new_max = jnp.maximum(old_max, jnp.max(scores, axis=1))
        factor = jnp.exp(old_max - new_max)
        weights = jnp.exp(scores - new_max[:, None])
        new_total = old_total * factor + jnp.sum(weights, axis=1)
        new_sum = old_sum * factor[:, None] + jnp.dot(
            weights.astype(jnp.bfloat16), value_part, preferred_element_type=jnp.float32
        )
        return (new_max, new_total, new_sum)

    return lax.map(
        per_head,
        (jnp.arange(head_total, dtype=jnp.int32), head_queries, running[0], running[1], running[2]),
    )


def finish(received):
    part_max, part_total, part_sum = received
    joint_max = jnp.max(part_max, axis=0)
    factor = jnp.exp(part_max - joint_max[None])
    total_sum = jnp.sum(part_total * factor, axis=0)
    summed = jnp.sum(part_sum * factor[..., None], axis=0)
    return summed / total_sum[..., None]


def starting(head_total, query_total):
    return (
        jnp.full((head_total, query_total), very_negative, jnp.float32),
        jnp.zeros((head_total, query_total), jnp.float32),
        jnp.zeros((head_total, query_total, DH), jnp.float32),
    )


def body(queries, keys, values, masked_at, mask_query, mask_key, mask_value):
    local_rows = queries.shape[0]
    full_width = queries.shape[1]
    first_row = lax.axis_index(("pb", "kv", "ha")) * local_rows
    positions = first_row + jnp.arange(local_rows, dtype=jnp.int32)
    masked_flags = jnp.any(positions[:, None] == masked_at[None, :], axis=1)
    query_used = jnp.where(masked_flags[:, None], rotated(mask_query, positions), queries)
    key_used = jnp.where(masked_flags[:, None], rotated(mask_key, positions), keys)
    value_used = jnp.where(masked_flags[:, None], mask_value[None, :], values)
    group_width = full_width // lax.axis_size("ha")
    head_total = group_width // DH
    score_scale = 1.0 / math.sqrt(DH)
    query_group, key_group, value_group = (
        lax.all_to_all(query_used, "ha", split_axis=1, concat_axis=0, tiled=True),
        lax.all_to_all(key_used, "ha", split_axis=1, concat_axis=0, tiled=True),
        lax.all_to_all(value_used, "ha", split_axis=1, concat_axis=0, tiled=True),
    )
    own_queries = lax.all_gather(query_group, "kv", axis=0, tiled=True)
    query_total = own_queries.shape[0]
    head_queries = own_queries.reshape(query_total, head_total, DH).transpose(1, 0, 2)
    portion = side_by_side((key_group, value_group), "pb", 0, 1)
    running = attend_piece(
        starting(head_total, query_total), head_queries, portion[0], portion[1], score_scale
    )
    owned_rows = query_total // lax.axis_size("kv")
    stacked = (running[0][None], running[1][None], running[2][None])
    normalized = finish(
        (
            lax.all_to_all(stacked[0], "kv", split_axis=2, concat_axis=0, tiled=True),
            lax.all_to_all(stacked[1], "kv", split_axis=2, concat_axis=0, tiled=True),
            lax.all_to_all(stacked[2], "kv", split_axis=2, concat_axis=0, tiled=True),
        )
    )
    out_rows = normalized.transpose(1, 0, 2).reshape(owned_rows, group_width).astype(jnp.bfloat16)
    return lax.all_to_all(out_rows, "ha", split_axis=0, concat_axis=1, tiled=True)


def solution(mesh):
    in_specs = (
        P(("pb", "kv", "ha"), None),
        P(("pb", "kv", "ha"), None),
        P(("pb", "kv", "ha"), None),
        P(),
        P(),
        P(),
        P(),
    )
    out_specs = P(("pb", "kv", "ha"), None)
    return jax.shard_map(body, mesh=mesh, in_specs=in_specs, out_specs=out_specs, check_vma=False)
```

profile of v0, /device:TPU:24, one launch (start us, length us, event | category | flops | bytes accessed | tf_op | source)
XLA Modules:
  0.0 589.7 jit_solution(16703127739279018998)
XLA Ops:
  6.6 0.7 bitcast_convert_fusion
  7.2 0.7 bitcast_convert_fusion.1
  8.9 1.0 compare_reduce_fusion
  10.2 1.5 bitcast_select_fusion
  11.7 13.1 %all_to_all.127 = bf16[96,2,1024]{2,0,1:T(8,128)(2,1)} all-to-all(bf16[96,2,1024]{2,0,1:T(8,128)(2,1)S(1)} %bitcast.98), channel_id=1, replica_groups=mesh['pb'=8,'kv'=8,'ha'=2] {'ha'}, dimensions={1} | all-to-all | bytes 786432 | tf_op jit(solution)/shard_map/all_to_all | solution.py:94
  24.9 0.8 copy.63
  25.6 3.5 all-to-all-start.2
  29.2 11.5 %all-to-all-done.2 = bf16[96,2,1024]{2,0,1:T(8,128)(2,1)S(1)} async-done(((bf16[96,2,1024]{2,0,1:T(8,128)(2,1)}), bf16[96,2,1024]{2,0,1:T(8,128)(2,1)S(1)}, u32[]{:S(2)}, u32[]{:S(2)}) %all-to-all-start.2) | async-done | bytes 393248 | tf_op jit(solution)/shard_map/all_to_all | solution.py:96
  40.7 29.5 %all_to_all.128 = bf16[96,2,1024]{2,0,1:T(8,128)(2,1)S(1)} all-to-all(bf16[96,2,1024]{2,0,1:T(8,128)(2,1)S(1)} %bitcast.97), channel_id=1, replica_groups=mesh['pb'=8,'kv'=8,'ha'=2] {'ha'}, dimensions={1} | all-to-all | bytes 786432 | tf_op jit(solution)/shard_map/all_to_all | solution.py:95
  70.2 1.0 pad_maximum_fusion
  71.3 4.7 copy.34
  76.0 35.1 %all-gather.5.cloned.1.call-done = bf16[1536,2048]{1,0:T(8,128)(2,1)} async-done(((bf16[192,2048]{1,0:T(8,128)(2,1)}), bf16[1536,2048]{1,0:T(8,128)(2,1)}) %all-gather.5.cloned.1.call-update) | async-done | bytes 6291472 | tf_op jit(solution)/shard_map/all_gather | solution.py:15
  111.0 6.1 %fusion.21 = (bf16[1536,1024]{1,0:T(8,128)(2,1)}, bf16[1536,1024]{1,0:T(8,128)(2,1)}) fusion(bf16[1536,2048]{1,0:T(8,128)(2,1)} %all-gather.5.cloned.1.call-done), kind=kLoop, calls=%fused_computation.47 | loop fusion | bytes 12582912 | tf_op jit(solution)/shard_map/slice | solution.py:17
  117.2 319.7 %while.14 = (s32[]{:T(128)}, f32[8,1536]{1,0:T(8,128)S(1)}, f32[8,1536]{1,0:T(8,128)S(1)}, f32[8,1536,128]{2,0,1:T(8,128)}, bf16[8,1536,128]{1,2,0:T(8,128)(2,1)...) while((s32[]{:T(128)}, f32[8,1536]{1,0:T(8,128)S(1)}, ...), condition=%wide.region_4.5_spmd, body=%wide.region_1.4_spmd.sunk | while | flops 1222318080 | bytes 31955152 | solution.py:58
  117.2 0.7 dynamic_slice.38
  118.6 6.1 %fusion.31 = (f32[1536]{0:T(1024)S(1)}, f32[1536,1536]{0,1:T(8,128)}) fusion(bf16[8,1536,128]{1,2,0:T(8,128)(2,1)} %get-tuple-element.212, s32[]{:T(128)S(6)} %copy.73, bf16[1536,1024]{1,0:T(8,128)(2,1)} %get-tuple-element.214, s32[]{:T(128)S(6)} %select_n.22), kind=kOutput, calls=%fused_computation.46.clone.1 | convolution fusion | flops 608696832 | bytes 10229768 | tf_op jit(solution)/shard_map/while/body/eval_jaxpr/qd,kd->qk/dot_general | solution.py:46
  124.9 5.0 fusion.32
  130.1 5.5 fusion.33
  135.6 21.6 %dynamic_update_slice.16 = f32[8,1536,128]{2,0,1:T(8,128)} dynamic-update-slice(f32[8,1536,128]{2,0,1:T(8,128)} %get-tuple-element.199, f32[1,1536,128]{2,0,1:T(1,128)S(1)} %bitcast.90, s32[]{:T(128)S(6)} %copy.73, s32[]{:T(128)} %constant.30.clone.1..sunk, s32[]{:T(128)} %constant.30.clone.1..sunk) | dynamic-update-slice | bytes 1572868 | tf_op jit(solution)/shard_map/while/body/jit(dynamic_update_index_in_dim)/dynamic_update_slice | solution.py:58
  157.2 0.7 dynamic_slice.38
  158.5 6.1 %fusion.31 = (f32[1536]{0:T(1024)S(1)}, f32[1536,1536]{0,1:T(8,128)}) fusion(bf16[8,1536,128]{1,2,0:T(8,128)(2,1)} %get-tuple-element.212, s32[]{:T(128)S(6)} %copy.73, bf16[1536,1024]{1,0:T(8,128)(2,1)} %get-tuple-element.214, s32[]{:T(128)S(6)} %select_n.22), kind=kOutput, calls=%fused_computation.46.clone.1 | convolution fusion | flops 608696832 | bytes 10229768 | tf_op jit(solution)/shard_map/while/body/eval_jaxpr/qd,kd->qk/dot_general | solution.py:46
  164.8 5.0 fusion.32
  170.0 5.5 fusion.33
  175.5 21.6 %dynamic_update_slice.16 = f32[8,1536,128]{2,0,1:T(8,128)} dynamic-update-slice(f32[8,1536,128]{2,0,1:T(8,128)} %get-tuple-element.199, f32[1,1536,128]{2,0,1:T(1,128)S(1)} %bitcast.90, s32[]{:T(128)S(6)} %copy.73, s32[]{:T(128)} %constant.30.clone.1..sunk, s32[]{:T(128)} %constant.30.clone.1..sunk) | dynamic-update-slice | bytes 1572868 | tf_op jit(solution)/shard_map/while/body/jit(dynamic_update_index_in_dim)/dynamic_update_slice | solution.py:58
  198.5 6.1 %fusion.31 = (f32[1536]{0:T(1024)S(1)}, f32[1536,1536]{0,1:T(8,128)}) fusion(bf16[8,1536,128]{1,2,0:T(8,128)(2,1)} %get-tuple-element.212, s32[]{:T(128)S(6)} %copy.73, bf16[1536,1024]{1,0:T(8,128)(2,1)} %get-tuple-element.214, s32[]{:T(128)S(6)} %select_n.22), kind=kOutput, calls=%fused_computation.46.clone.1 | convolution fusion | flops 608696832 | bytes 10229768 | tf_op jit(solution)/shard_map/while/body/eval_jaxpr/qd,kd->qk/dot_general | solution.py:46
  204.8 5.0 fusion.32
  210.0 5.5 fusion.33
  215.5 21.6 %dynamic_update_slice.16 = f32[8,1536,128]{2,0,1:T(8,128)} dynamic-update-slice(f32[8,1536,128]{2,0,1:T(8,128)} %get-tuple-element.199, f32[1,1536,128]{2,0,1:T(1,128)S(1)} %bitcast.90, s32[]{:T(128)S(6)} %copy.73, s32[]{:T(128)} %constant.30.clone.1..sunk, s32[]{:T(128)} %constant.30.clone.1..sunk) | dynamic-update-slice | bytes 1572868 | tf_op jit(solution)/shard_map/while/body/jit(dynamic_update_index_in_dim)/dynamic_update_slice | solution.py:58
  237.1 0.7 dynamic_slice.38
  238.5 6.1 %fusion.31 = (f32[1536]{0:T(1024)S(1)}, f32[1536,1536]{0,1:T(8,128)}) fusion(bf16[8,1536,128]{1,2,0:T(8,128)(2,1)} %get-tuple-element.212, s32[]{:T(128)S(6)} %copy.73, bf16[1536,1024]{1,0:T(8,128)(2,1)} %get-tuple-element.214, s32[]{:T(128)S(6)} %select_n.22), kind=kOutput, calls=%fused_computation.46.clone.1 | convolution fusion | flops 608696832 | bytes 10229768 | tf_op jit(solution)/shard_map/while/body/eval_jaxpr/qd,kd->qk/dot_general | solution.py:46
  244.8 5.0 fusion.32
  249.9 5.5 fusion.33
  255.5 21.6 %dynamic_update_slice.16 = f32[8,1536,128]{2,0,1:T(8,128)} dynamic-update-slice(f32[8,1536,128]{2,0,1:T(8,128)} %get-tuple-element.199, f32[1,1536,128]{2,0,1:T(1,128)S(1)} %bitcast.90, s32[]{:T(128)S(6)} %copy.73, s32[]{:T(128)} %constant.30.clone.1..sunk, s32[]{:T(128)} %constant.30.clone.1..sunk) | dynamic-update-slice | bytes 1572868 | tf_op jit(solution)/shard_map/while/body/jit(dynamic_update_index_in_dim)/dynamic_update_slice | solution.py:58
  278.4 6.1 %fusion.31 = (f32[1536]{0:T(1024)S(1)}, f32[1536,1536]{0,1:T(8,128)}) fusion(bf16[8,1536,128]{1,2,0:T(8,128)(2,1)} %get-tuple-element.212, s32[]{:T(128)S(6)} %copy.73, bf16[1536,1024]{1,0:T(8,128)(2,1)} %get-tuple-element.214, s32[]{:T(128)S(6)} %select_n.22), kind=kOutput, calls=%fused_computation.46.clone.1 | convolution fusion | flops 608696832 | bytes 10229768 | tf_op jit(solution)/shard_map/while/body/eval_jaxpr/qd,kd->qk/dot_general | solution.py:46
  284.7 5.0 fusion.32
  289.9 5.5 fusion.33
  295.4 21.6 %dynamic_update_slice.16 = f32[8,1536,128]{2,0,1:T(8,128)} dynamic-update-slice(f32[8,1536,128]{2,0,1:T(8,128)} %get-tuple-element.199, f32[1,1536,128]{2,0,1:T(1,128)S(1)} %bitcast.90, s32[]{:T(128)S(6)} %copy.73, s32[]{:T(128)} %constant.30.clone.1..sunk, s32[]{:T(128)} %constant.30.clone.1..sunk) | dynamic-update-slice | bytes 1572868 | tf_op jit(solution)/shard_map/while/body/jit(dynamic_update_index_in_dim)/dynamic_update_slice | solution.py:58
  317.0 0.7 dynamic_slice.38
  318.4 6.1 %fusion.31 = (f32[1536]{0:T(1024)S(1)}, f32[1536,1536]{0,1:T(8,128)}) fusion(bf16[8,1536,128]{1,2,0:T(8,128)(2,1)} %get-tuple-element.212, s32[]{:T(128)S(6)} %copy.73, bf16[1536,1024]{1,0:T(8,128)(2,1)} %get-tuple-element.214, s32[]{:T(128)S(6)} %select_n.22), kind=kOutput, calls=%fused_computation.46.clone.1 | convolution fusion | flops 608696832 | bytes 10229768 | tf_op jit(solution)/shard_map/while/body/eval_jaxpr/qd,kd->qk/dot_general | solution.py:46
  324.7 5.0 fusion.32
  329.9 5.6 fusion.33
  335.4 21.6 %dynamic_update_slice.16 = f32[8,1536,128]{2,0,1:T(8,128)} dynamic-update-slice(f32[8,1536,128]{2,0,1:T(8,128)} %get-tuple-element.199, f32[1,1536,128]{2,0,1:T(1,128)S(1)} %bitcast.90, s32[]{:T(128)S(6)} %copy.73, s32[]{:T(128)} %constant.30.clone.1..sunk, s32[]{:T(128)} %constant.30.clone.1..sunk) | dynamic-update-slice | bytes 1572868 | tf_op jit(solution)/shard_map/while/body/jit(dynamic_update_index_in_dim)/dynamic_update_slice | solution.py:58
  358.4 6.1 %fusion.31 = (f32[1536]{0:T(1024)S(1)}, f32[1536,1536]{0,1:T(8,128)}) fusion(bf16[8,1536,128]{1,2,0:T(8,128)(2,1)} %get-tuple-element.212, s32[]{:T(128)S(6)} %copy.73, bf16[1536,1024]{1,0:T(8,128)(2,1)} %get-tuple-element.214, s32[]{:T(128)S(6)} %select_n.22), kind=kOutput, calls=%fused_computation.46.clone.1 | convolution fusion | flops 608696832 | bytes 10229768 | tf_op jit(solution)/shard_map/while/body/eval_jaxpr/qd,kd->qk/dot_general | solution.py:46
  364.7 5.0 fusion.32
  369.9 5.5 fusion.33
  375.4 21.6 %dynamic_update_slice.16 = f32[8,1536,128]{2,0,1:T(8,128)} dynamic-update-slice(f32[8,1536,128]{2,0,1:T(8,128)} %get-tuple-element.199, f32[1,1536,128]{2,0,1:T(1,128)S(1)} %bitcast.90, s32[]{:T(128)S(6)} %copy.73, s32[]{:T(128)} %constant.30.clone.1..sunk, s32[]{:T(128)} %constant.30.clone.1..sunk) | dynamic-update-slice | bytes 1572868 | tf_op jit(solution)/shard_map/while/body/jit(dynamic_update_index_in_dim)/dynamic_update_slice | solution.py:58
  398.3 6.1 %fusion.31 = (f32[1536]{0:T(1024)S(1)}, f32[1536,1536]{0,1:T(8,128)}) fusion(bf16[8,1536,128]{1,2,0:T(8,128)(2,1)} %get-tuple-element.212, s32[]{:T(128)S(6)} %copy.73, bf16[1536,1024]{1,0:T(8,128)(2,1)} %get-tuple-element.214, s32[]{:T(128)S(6)} %select_n.22), kind=kOutput, calls=%fused_computation.46.clone.1 | convolution fusion | flops 608696832 | bytes 10229768 | tf_op jit(solution)/shard_map/while/body/eval_jaxpr/qd,kd->qk/dot_general | solution.py:46
  404.6 5.0 fusion.32
  409.8 5.5 fusion.33
  415.3 21.6 %dynamic_update_slice.16 = f32[8,1536,128]{2,0,1:T(8,128)} dynamic-update-slice(f32[8,1536,128]{2,0,1:T(8,128)} %get-tuple-element.199, f32[1,1536,128]{2,0,1:T(1,128)S(1)} %bitcast.90, s32[]{:T(128)S(6)} %copy.73, s32[]{:T(128)} %constant.30.clone.1..sunk, s32[]{:T(128)} %constant.30.clone.1..sunk) | dynamic-update-slice | bytes 1572868 | tf_op jit(solution)/shard_map/while/body/jit(dynamic_update_index_in_dim)/dynamic_update_slice | solution.py:58
  437.7 7.1 %reduce.1 = f32[1536,8]{1,0:T(8,128)S(1)} reduce(f32[1536,1,8]{2,1,0:T(1,128)S(1)} %bitcast.92, f32[]{:T(128)} %broadcast.133), dimensions={1}, to_apply=%bitcast.76.reduce_sub_computation | reduce | bytes 98308
  444.8 1.0 reshape.158
  445.8 5.8 all-to-all-start.5
  451.9 7.1 %reduce.3 = f32[1536,8]{1,0:T(8,128)S(1)} reduce(f32[1536,1,8]{2,1,0:T(1,128)S(1)} %bitcast.93, f32[]{:T(128)} %broadcast.133), dimensions={1}, to_apply=%bitcast.74.reduce_sub_computation | reduce | bytes 98308
  459.4 9.8 %all_to_all.129 = f32[8,1,1536]{2,1,0:T(1,128)S(1)} all-to-all(f32[8,1,1536]{2,1,0:T(1,128)S(1)} %reshape.156), channel_id=1, replica_groups=mesh['pb'=8,'kv'=8,'ha'=2] {'kv'}, dimensions={0} | all-to-all | bytes 98304 | tf_op jit(solution)/shard_map/all_to_all | solution.py:109
  469.2 6.6 %all-to-all-start.3 = ((f32[1,8,1536,128]{3,1,0,2:T(8,128)}), f32[1,8,1536,128]{3,1,0,2:T(8,128)}, u32[]{:S(2)}, u32[]{:S(2)}) async-start(f32[1,8,1536,128]{3,1,0,2:T(8,128)} %bitcast.91), calls=%async_computation.3 | async-start | bytes 12582912 | tf_op jit(solution)/shard_map/all_to_all | solution.py:111
  475.8 0.7 reduce.2
  476.5 1.2 reshape.159
  478.0 0.7 reduce.4
  478.8 1.2 reshape.157
  480.4 84.7 %all-to-all-done.3 = f32[1,8,1536,128]{3,1,0,2:T(8,128)} async-done(((f32[1,8,1536,128]{3,1,0,2:T(8,128)}), f32[1,8,1536,128]{3,1,0,2:T(8,128)}, u32[]{:S(2)}, u32[]{:S(2)}) %all-to-all-start.3) | async-done | bytes 6291488 | tf_op jit(solution)/shard_map/all_to_all | solution.py:111
  565.0 5.0 fusion.14
  570.8 11.4 %all_to_all.130 = bf16[2,96,1024]{2,1,0:T(8,128)(2,1)S(1)} all-to-all(bf16[2,96,1024]{2,1,0:T(8,128)(2,1)S(1)} %convert_element_type.32), channel_id=1, replica_groups=mesh['pb'=8,'kv'=8,'ha'=2] {'ha'}, dimensions={0} | all-to-all | bytes 786432 | tf_op jit(solution)/shard_map/all_to_all | solution.py:115
  582.1 0.8 copy.54
  (74 shorter events, 9.6 us)
Async XLA Ops:
  6.5 64.7 %all-gather.3.cloned.1.call-start = ((), (), s32[]{:S(2)}) async-start(), calls=%async_computation.7 | async-start | bytes 3538944 | tf_op jit(solution)/shard_map/all_gather | solution.py:98
  25.6 15.1 %all-to-all-start.2 = ((bf16[96,2,1024]{2,0,1:T(8,128)(2,1)}), bf16[96,2,1024]{2,0,1:T(8,128)(2,1)S(1)}, u32[]{:S(2)}, u32[]{:S(2)}) async-start(bf16[96,2,1024]{2,0,1:T(8,128)(2,1)} %bitcast.81), calls=%async_computation.2 | async-start | bytes 786432 | tf_op jit(solution)/shard_map/all_to_all | solution.py:96
  29.1 81.9 %all-gather.5.cloned.1.call-start = ((), (), s32[]{:S(2)}) async-start(), calls=%async_computation.8 | async-start | bytes 7077888 | tf_op jit(solution)/shard_map/all_gather | solution.py:15
  445.8 13.6 %all-to-all-start.5 = ((f32[8,1,1536]{2,1,0:T(1,128)}), f32[8,1,1536]{2,1,0:T(1,128)S(1)}, u32[]{:S(2)}, u32[]{:S(2)}) async-start(f32[8,1,1536]{2,1,0:T(1,128)} %reshape.158), calls=%async_computation.5 | async-start | bytes 98304 | tf_op jit(solution)/shard_map/all_to_all | solution.py:110
  469.2 95.9 %all-to-all-start.3 = ((f32[1,8,1536,128]{3,1,0,2:T(8,128)}), f32[1,8,1536,128]{3,1,0,2:T(8,128)}, u32[]{:S(2)}, u32[]{:S(2)}) async-start(f32[1,8,1536,128]{3,1,0,2:T(8,128)} %bitcast.91), calls=%async_computation.3 | async-start | bytes 12582912 | tf_op jit(solution)/shard_map/all_to_all | solution.py:111
Sparse Core Ops, SparseCore 0:
  25.0 41.8 all-gather.2
  71.3 39.6 all-gather.4
where the time goes:
time: 595 us; the launch traced here: 590 us
  local copies, waits for them, and re-layouts  199 us (33%)
  waiting for transfers between devices  131 us (22%)
  matrix products  93.2 us (16%)
  other arithmetic  67 us (11%)
  blocking collectives  63.8 us (11%)
  starting transfers between devices  15.9 us (3%)
  between operations  13.6 us (2%)
    dynamic_update_slice x24, local copies, waits for them, and re-layouts, attend_piece(): lax.map(per_head, (jnp.arange(head_total, dtype=jnp.int32), head_queries,...  175 us
    all_to_all x1, waiting for transfers between devices, body(): lax.all_to_all(stacked[2], 'kv', split_axis=2, concat_axis=0, tiled=True)  84.7 us
    dot_general x8, matrix products, per_head(): jnp.einsum('qd,kd->qk', query_part, key_part, preferred_element_type=jnp....  49.1 us
    dot_general x8, matrix products, per_head(): jnp.dot(weights.astype(jnp.bfloat16), value_part, preferred_element_type=...  44.2 us
    reduce_sum x8, other arithmetic, per_head(): new_total = old_total * factor + jnp.sum(weights, axis=1)  39.9 us
    all_gather x1, waiting for transfers between devices, side_by_side(): lax.all_gather(both, axis, axis=dim, tiled=True)  35.1 us
    all_to_all x1, blocking collectives, body(): lax.all_to_all(key_used, 'ha', split_axis=1, concat_axis=0, tiled=True)  29.5 us
    unnamed x2, other arithmetic  14.2 us
  transfers between devices with their start and end apart: 5, of which 3 were waited for; matrix products, arithmetic and copies ran while one was open for 3% of the time, Pallas kernels for 0%

commit v1 on v0

--- a/solution.py
+++ b/solution.py
@@ -108,7 +108,12 @@
         (
             lax.all_to_all(stacked[0], "kv", split_axis=2, concat_axis=0, tiled=True),
             lax.all_to_all(stacked[1], "kv", split_axis=2, concat_axis=0, tiled=True),
-            lax.all_to_all(stacked[2], "kv", split_axis=2, concat_axis=0, tiled=True),
+            jnp.concatenate(
+                lax.all_to_all(
+                    jnp.stack(jnp.split(stacked[2], lax.axis_size("kv"), axis=2)), "kv", 0, 0
+                ),
+                axis=0,
+            ),
         )
     )
     out_rows = normalized.transpose(1, 0, 2).reshape(owned_rows, group_width).astype(jnp.bfloat16)

time: 595 us -> 361 us (0.61)
  local copies, waits for them, and re-layouts: 199 us -> 41.7 us
  matrix products: 93.2 us -> 50.2 us
  other arithmetic: 67 us -> 37.7 us
  blocking collectives: 63.8 us -> 53.9 us
    dynamic_update_slice x24 -> x16, local copies, waits for them, and re-layouts: 175 us -> 2.52 us  [attend_piece(): lax.map(per_head, (jnp.arange(head_total, dtype=jnp.int32), head_queries,...]
    dot_general x8, matrix products: 49.1 us -> 19.1 us  [per_head(): jnp.einsum('qd,kd->qk', query_part, key_part, preferred_element_type=jnp....]
    reduce_sum x8, other arithmetic: 39.9 us -> 10.6 us  [per_head(): new_total = old_total * factor + jnp.sum(weights, axis=1)]
    unnamed x5 -> x12, local copies, waits for them, and re-layouts: 4.4 us -> 19.8 us
    dot_general x8, matrix products: 44.2 us -> 31.1 us  [per_head(): jnp.dot(weights.astype(jnp.bfloat16), value_part, preferred_element_type=...]
    all_to_all x2 -> x1, blocking collectives: 39.3 us -> 29.5 us  [body(): lax.all_to_all(value_used, 'ha', split_axis=1, concat_axis=0, tiled=True)]
    all_to_all x2 -> x3, starting transfers between devices: 10.1 us -> 15.9 us  [the longest x1 6.63 us: body(): lax.all_to_all(jnp.stack(jnp.split(stacked[2], lax.axis_size('kv'), axis=...]
    all_to_all x2 -> x3, waiting for transfers between devices: 96.2 us -> 96.2 us  [the longest x1 84.7 us: body(): lax.all_to_all(jnp.stack(jnp.split(stacked[2], lax.axis_size('kv'), axis=...]
  transfers between devices with their start and end apart: 5 -> 6, of which waited for: 3 -> 4; matrix products, arithmetic and copies ran while one was open for 3% -> 10% of each run, Pallas kernels for 0% -> 0%
where the time goes in v1:
time: 361 us; the launch traced here: 359 us
  waiting for transfers between devices  135 us (37%)
  blocking collectives  53.9 us (15%)
  matrix products  50.2 us (14%)
  local copies, waits for them, and re-layouts  41.7 us (12%)
  other arithmetic  37.7 us (10%)
  starting transfers between devices  21.6 us (6%)
  between operations  13.6 us (4%)
  loops' own time  5.11 us (1%)
    all_to_all x1, waiting for transfers between devices, body(): lax.all_to_all(jnp.stack(jnp.split(stacked[2], lax.axis_size('kv'), axis=...  84.7 us
    all_gather x1, waiting for transfers between devices, side_by_side(): lax.all_gather(both, axis, axis=dim, tiled=True)  36.6 us
    dot_general x8, matrix products, per_head(): jnp.dot(weights.astype(jnp.bfloat16), value_part, preferred_element_type=...  31.1 us
    all_to_all x1, blocking collectives, body(): lax.all_to_all(value_used, 'ha', split_axis=1, concat_axis=0, tiled=True)  29.5 us
    unnamed x12, local copies, waits for them, and re-layouts  19.8 us
    dot_general x8, matrix products, per_head(): jnp.einsum('qd,kd->qk', query_part, key_part, preferred_element_type=jnp....  19.1 us
    unnamed x2, other arithmetic  14.4 us
    all_to_all x1, blocking collectives, body(): lax.all_to_all(query_used, 'ha', split_axis=1, concat_axis=0, tiled=True)  13.1 us
  transfers between devices with their start and end apart: 6, of which 4 were waited for; matrix products, arithmetic and copies ran while one was open for 10% of the time, Pallas kernels for 0%

profile of v1, /device:TPU:24, one launch (start us, length us, event | category | flops | bytes accessed | tf_op | source)
XLA Modules:
  0.0 358.9 jit_solution(6360371607480611116)
XLA Ops:
  6.6 0.7 bitcast_convert_fusion
  7.3 0.7 bitcast_convert_fusion.1
  9.1 1.0 compare_reduce_fusion
  10.2 1.5 bitcast_select_fusion
  11.7 13.1 %all_to_all.114 = bf16[96,2,1024]{2,0,1:T(8,128)(2,1)} all-to-all(bf16[96,2,1024]{2,0,1:T(8,128)(2,1)S(1)} %bitcast.127), channel_id=1, replica_groups=mesh['pb'=8,'kv'=8,'ha'=2] {'ha'}, dimensions={1} | all-to-all | bytes 786432 | tf_op jit(solution)/shard_map/all_to_all | solution.py:94
  24.9 0.8 copy.61
  25.6 3.5 all-to-all-start.1
  29.2 11.5 %all-to-all-done.1 = bf16[96,2,1024]{2,0,1:T(8,128)(2,1)S(1)} async-done(((bf16[96,2,1024]{2,0,1:T(8,128)(2,1)}), bf16[96,2,1024]{2,0,1:T(8,128)(2,1)S(1)}, u32[]{:S(2)}, u32[]{:S(2)}) %all-to-all-start.1) | async-done | bytes 393248 | tf_op jit(solution)/shard_map/all_to_all | solution.py:95
  40.7 29.5 %all_to_all.115 = bf16[96,2,1024]{2,0,1:T(8,128)(2,1)S(1)} all-to-all(bf16[96,2,1024]{2,0,1:T(8,128)(2,1)S(1)} %bitcast.126), channel_id=1, replica_groups=mesh['pb'=8,'kv'=8,'ha'=2] {'ha'}, dimensions={1} | all-to-all | bytes 786432 | tf_op jit(solution)/shard_map/all_to_all | solution.py:96
  70.2 1.0 pad_maximum_fusion
  71.3 3.2 copy.38
  74.5 36.6 %all-gather.5.cloned.1.call-done = bf16[1536,2048]{1,0:T(8,128)(2,1)} async-done(((bf16[192,2048]{1,0:T(8,128)(2,1)}), bf16[1536,2048]{1,0:T(8,128)(2,1)}) %all-gather.5.cloned.1.call-update) | async-done | bytes 6291472 | tf_op jit(solution)/shard_map/all_gather | solution.py:15
  111.1 6.2 %fusion.35 = (bf16[1536,1024]{1,0:T(8,128)(2,1)}, bf16[1536,1024]{1,0:T(8,128)(2,1)}) fusion(bf16[1536,2048]{1,0:T(8,128)(2,1)} %all-gather.5.cloned.1.call-done), kind=kLoop, calls=%fused_computation.65 | loop fusion | bytes 12582912 | tf_op jit(solution)/shard_map/slice | solution.py:17
  117.2 73.4 %while.14 = (s32[]{:T(128)}, f32[8,1536]{1,0:T(8,128)S(1)}, f32[8,1536]{1,0:T(8,128)S(1)}, f32[8,1536,128]{2,1,0:T(8,128)}, bf16[8,1536,128]{1,2,0:T(8,128)(2,1)...) while((s32[]{:T(128)}, f32[8,1536]{1,0:T(8,128)S(1)}, ...), condition=%wide.region_4.5_spmd, body=%wide.region_1.4_spmd.sunk | while | flops 1222318080 | bytes 30383296 | solution.py:58
  118.4 2.4 fusion.45
  120.8 3.9 %fusion.47 = f32[8,1536,128]{2,1,0:T(8,128)} fusion(f32[8,1536,128]{2,1,0:T(8,128)} %get-tuple-element.199, s32[]{:T(128)} %get-tuple-element.196, f32[1536,1536]{0,1:T(8,128)S(1)} %get-tuple-element.182, f32[1536]{0:T(1024)S(1)} %get-tuple-element.181, bf16[1536,1024]{1,0:T(8,128)(2,1)} %get-tuple-element.215, s32[]{:T(128)S(6)} %select_n.22, ...), kind=kOutput, calls=%fused_computation.8.clone.1 | convolution fusion | flops 608894976 | bytes 10629636 | tf_op jit(solution)/shard_map/while/body/eval_jaxpr/dot_general | solution.py:53
  124.7 1.3 fusion.46
  127.6 2.4 fusion.45
  130.0 3.9 %fusion.47 = f32[8,1536,128]{2,1,0:T(8,128)} fusion(f32[8,1536,128]{2,1,0:T(8,128)} %get-tuple-element.199, s32[]{:T(128)} %get-tuple-element.196, f32[1536,1536]{0,1:T(8,128)S(1)} %get-tuple-element.182, f32[1536]{0:T(1024)S(1)} %get-tuple-element.181, bf16[1536,1024]{1,0:T(8,128)(2,1)} %get-tuple-element.215, s32[]{:T(128)S(6)} %select_n.22, ...), kind=kOutput, calls=%fused_computation.8.clone.1 | convolution fusion | flops 608894976 | bytes 10629636 | tf_op jit(solution)/shard_map/while/body/eval_jaxpr/dot_general | solution.py:53
  133.9 1.3 fusion.46
  135.6 0.6 dynamic_slice.38
  136.7 2.4 fusion.45
  139.2 3.9 %fusion.47 = f32[8,1536,128]{2,1,0:T(8,128)} fusion(f32[8,1536,128]{2,1,0:T(8,128)} %get-tuple-element.199, s32[]{:T(128)} %get-tuple-element.196, f32[1536,1536]{0,1:T(8,128)S(1)} %get-tuple-element.182, f32[1536]{0:T(1024)S(1)} %get-tuple-element.181, bf16[1536,1024]{1,0:T(8,128)(2,1)} %get-tuple-element.215, s32[]{:T(128)S(6)} %select_n.22, ...), kind=kOutput, calls=%fused_computation.8.clone.1 | convolution fusion | flops 608894976 | bytes 10629636 | tf_op jit(solution)/shard_map/while/body/eval_jaxpr/dot_general | solution.py:53
  143.0 1.3 fusion.46
  145.9 2.4 fusion.45
  148.3 3.9 %fusion.47 = f32[8,1536,128]{2,1,0:T(8,128)} fusion(f32[8,1536,128]{2,1,0:T(8,128)} %get-tuple-element.199, s32[]{:T(128)} %get-tuple-element.196, f32[1536,1536]{0,1:T(8,128)S(1)} %get-tuple-element.182, f32[1536]{0:T(1024)S(1)} %get-tuple-element.181, bf16[1536,1024]{1,0:T(8,128)(2,1)} %get-tuple-element.215, s32[]{:T(128)S(6)} %select_n.22, ...), kind=kOutput, calls=%fused_computation.8.clone.1 | convolution fusion | flops 608894976 | bytes 10629636 | tf_op jit(solution)/shard_map/while/body/eval_jaxpr/dot_general | solution.py:53
  152.2 1.3 fusion.46
  155.1 2.4 fusion.45
  157.5 3.9 %fusion.47 = f32[8,1536,128]{2,1,0:T(8,128)} fusion(f32[8,1536,128]{2,1,0:T(8,128)} %get-tuple-element.199, s32[]{:T(128)} %get-tuple-element.196, f32[1536,1536]{0,1:T(8,128)S(1)} %get-tuple-element.182, f32[1536]{0:T(1024)S(1)} %get-tuple-element.181, bf16[1536,1024]{1,0:T(8,128)(2,1)} %get-tuple-element.215, s32[]{:T(128)S(6)} %select_n.22, ...), kind=kOutput, calls=%fused_computation.8.clone.1 | convolution fusion | flops 608894976 | bytes 10629636 | tf_op jit(solution)/shard_map/while/body/eval_jaxpr/dot_general | solution.py:53
  161.4 1.3 fusion.46
  164.3 2.4 fusion.45
  166.7 3.9 %fusion.47 = f32[8,1536,128]{2,1,0:T(8,128)} fusion(f32[8,1536,128]{2,1,0:T(8,128)} %get-tuple-element.199, s32[]{:T(128)} %get-tuple-element.196, f32[1536,1536]{0,1:T(8,128)S(1)} %get-tuple-element.182, f32[1536]{0:T(1024)S(1)} %get-tuple-element.181, bf16[1536,1024]{1,0:T(8,128)(2,1)} %get-tuple-element.215, s32[]{:T(128)S(6)} %select_n.22, ...), kind=kOutput, calls=%fused_computation.8.clone.1 | convolution fusion | flops 608894976 | bytes 10629636 | tf_op jit(solution)/shard_map/while/body/eval_jaxpr/dot_general | solution.py:53
  170.5 1.3 fusion.46
  173.4 2.4 fusion.45
  175.8 3.9 %fusion.47 = f32[8,1536,128]{2,1,0:T(8,128)} fusion(f32[8,1536,128]{2,1,0:T(8,128)} %get-tuple-element.199, s32[]{:T(128)} %get-tuple-element.196, f32[1536,1536]{0,1:T(8,128)S(1)} %get-tuple-element.182, f32[1536]{0:T(1024)S(1)} %get-tuple-element.181, bf16[1536,1024]{1,0:T(8,128)(2,1)} %get-tuple-element.215, s32[]{:T(128)S(6)} %select_n.22, ...), kind=kOutput, calls=%fused_computation.8.clone.1 | convolution fusion | flops 608894976 | bytes 10629636 | tf_op jit(solution)/shard_map/while/body/eval_jaxpr/dot_general | solution.py:53
  179.7 1.3 fusion.46
  182.6 2.4 fusion.45
  185.0 3.9 %fusion.47 = f32[8,1536,128]{2,1,0:T(8,128)} fusion(f32[8,1536,128]{2,1,0:T(8,128)} %get-tuple-element.199, s32[]{:T(128)} %get-tuple-element.196, f32[1536,1536]{0,1:T(8,128)S(1)} %get-tuple-element.182, f32[1536]{0:T(1024)S(1)} %get-tuple-element.181, bf16[1536,1024]{1,0:T(8,128)(2,1)} %get-tuple-element.215, s32[]{:T(128)S(6)} %select_n.22, ...), kind=kOutput, calls=%fused_computation.8.clone.1 | convolution fusion | flops 608894976 | bytes 10629636 | tf_op jit(solution)/shard_map/while/body/eval_jaxpr/dot_general | solution.py:53
  188.9 1.3 fusion.46
  190.9 0.6 broadcast.133
  191.5 7.2 %reduce.3 = f32[1536,8]{1,0:T(8,128)S(1)} reduce(f32[1536,1,8]{2,1,0:T(1,128)S(1)} %bitcast.121, f32[]{:T(128)} %broadcast.133), dimensions={1}, to_apply=%bitcast.104.reduce_sub_computation | reduce | bytes 98308
  198.7 1.0 reshape.160
  199.7 5.8 %all-to-all-start.4 = ((f32[8,1,1536]{2,1,0:T(1,128)}), f32[8,1,1536]{2,1,0:T(1,128)S(1)}, u32[]{:S(2)}, u32[]{:S(2)}) async-start(f32[8,1,1536]{2,1,0:T(1,128)} %reshape.160), calls=%async_computation.4 | async-start | bytes 98304 | tf_op jit(solution)/shard_map/all_to_all | solution.py:109
  205.5 2.1 fusion.28
  207.6 2.1 fusion.27
  209.6 2.1 fusion.26
  211.8 2.2 fusion.25
  213.9 2.1 fusion.24
  216.0 2.1 fusion.23
  218.1 2.1 fusion.22
  220.5 7.2 %reduce.1 = f32[1536,8]{1,0:T(8,128)S(1)} reduce(f32[1536,1,8]{2,1,0:T(1,128)S(1)} %bitcast.122, f32[]{:T(128)} %broadcast.133), dimensions={1}, to_apply=%bitcast.106.reduce_sub_computation | reduce | bytes 98308
  227.7 1.0 reshape.162
  228.7 5.7 %all-to-all-start.5 = ((f32[8,1,1536]{2,1,0:T(1,128)}), f32[8,1,1536]{2,1,0:T(1,128)S(1)}, u32[]{:S(2)}, u32[]{:S(2)}) async-start(f32[8,1,1536]{2,1,0:T(1,128)} %reshape.162), calls=%async_computation.5 | async-start | bytes 98304 | tf_op jit(solution)/shard_map/all_to_all | solution.py:110
  234.4 2.1 fusion.21
  236.5 2.2 all-to-all-done.5
  238.7 6.6 %all-to-all-start.3 = ((f32[8,1,8,192,128]{4,3,2,1,0:T(8,128)}), f32[8,1,8,192,128]{4,3,2,1,0:T(8,128)}, u32[]{:S(2)}, u32[]{:S(2)}) async-start(f32[8,1,8,192,128]{4,3,2,1,0:T(8,128)} %fusion.21), calls=%async_computation.3 | async-start | bytes 12582912 | tf_op jit(solution)/shard_map/all_to_all | solution.py:112
  245.4 0.8 reduce.4
  246.2 1.2 reshape.161
  247.7 0.8 reduce.2
  248.5 1.2 reshape.163
  250.1 84.7 %all-to-all-done.3 = f32[8,1,8,192,128]{4,3,2,1,0:T(8,128)} async-done(((f32[8,1,8,192,128]{4,3,2,1,0:T(8,128)}), f32[8,1,8,192,128]{4,3,2,1,0:T(8,128)}, u32[]{:S(2)}, u32[]{:S(2)}) %all-to-all-start.3) | async-done | bytes 6291488 | tf_op jit(solution)/shard_map/all_to_all | solution.py:112
  334.8 4.5 %fusion.20 = f32[8,192,128]{2,1,0:T(8,128)S(1)} fusion(f32[8,1,8,192,128]{4,3,2,1,0:T(8,128)} %all-to-all-done.3, f32[8,8,192]{2,1,0:T(8,128)S(1)} %get-tuple-element.101), kind=kLoop, calls=%fused_computation.19 | loop fusion | flops 2949120 | bytes 7127040 | tf_op jit(solution)/shard_map/reduce_sum | solution.py:69
  340.0 11.2 %all_to_all.116 = bf16[2,96,1024]{2,1,0:T(8,128)(2,1)S(1)} all-to-all(bf16[2,96,1024]{2,1,0:T(8,128)(2,1)S(1)} %convert_element_type.32), channel_id=1, replica_groups=mesh['pb'=8,'kv'=8,'ha'=2] {'ha'}, dimensions={0} | all-to-all | bytes 786432 | tf_op jit(solution)/shard_map/all_to_all | solution.py:120
  351.2 0.8 copy.52
  (75 shorter events, 10.1 us)
Async XLA Ops:
  6.5 64.7 %all-gather.3.cloned.1.call-start = ((), (), s32[]{:S(2)}) async-start(), calls=%async_computation.7 | async-start | bytes 3538944 | tf_op jit(solution)/shard_map/all_gather | solution.py:98
  25.6 15.1 %all-to-all-start.1 = ((bf16[96,2,1024]{2,0,1:T(8,128)(2,1)}), bf16[96,2,1024]{2,0,1:T(8,128)(2,1)S(1)}, u32[]{:S(2)}, u32[]{:S(2)}) async-start(bf16[96,2,1024]{2,0,1:T(8,128)(2,1)} %bitcast.112), calls=%async_computation.1 | async-start | bytes 786432 | tf_op jit(solution)/shard_map/all_to_all | solution.py:95
  29.1 81.9 %all-gather.5.cloned.1.call-start = ((), (), s32[]{:S(2)}) async-start(), calls=%async_computation.8 | async-start | bytes 7077888 | tf_op jit(solution)/shard_map/all_gather | solution.py:15
  199.7 29.0 %all-to-all-start.4 = ((f32[8,1,1536]{2,1,0:T(1,128)}), f32[8,1,1536]{2,1,0:T(1,128)S(1)}, u32[]{:S(2)}, u32[]{:S(2)}) async-start(f32[8,1,1536]{2,1,0:T(1,128)} %reshape.160), calls=%async_computation.4 | async-start | bytes 98304 | tf_op jit(solution)/shard_map/all_to_all | solution.py:109
  228.7 10.0 %all-to-all-start.5 = ((f32[8,1,1536]{2,1,0:T(1,128)}), f32[8,1,1536]{2,1,0:T(1,128)S(1)}, u32[]{:S(2)}, u32[]{:S(2)}) async-start(f32[8,1,1536]{2,1,0:T(1,128)} %reshape.162), calls=%async_computation.5 | async-start | bytes 98304 | tf_op jit(solution)/shard_map/all_to_all | solution.py:110
  238.7 96.0 %all-to-all-start.3 = ((f32[8,1,8,192,128]{4,3,2,1,0:T(8,128)}), f32[8,1,8,192,128]{4,3,2,1,0:T(8,128)}, u32[]{:S(2)}, u32[]{:S(2)}) async-start(f32[8,1,8,192,128]{4,3,2,1,0:T(8,128)} %fusion.21), calls=%async_computation.3 | async-start | bytes 12582912 | tf_op jit(solution)/shard_map/all_to_all | solution.py:112
Sparse Core Ops, SparseCore 0:
  25.0 41.8 all-gather.2
  71.3 39.6 all-gather.4
